TPU v7x, 256 devices: a whole 4x4x8 slice. The times are simulated.
256 devices in a mesh: pp: 4 (over x_hi, core), tp: 16 (over z, x_lo), dp: 4 (over y).
Axes of the slice: x: 4 (x_hi: 2, x_lo: 2; x = x_hi * 2 + x_lo), y: 4, z: 8, core: 2. Of those that a mesh axis runs over, the one named last changes fastest.
Arguments:
- layer_input: bfloat16 [4, 4, 128, 4096], P('pp', 'dp', 'tp'), may hold values from -4 to 4
- gate_pre: bfloat16 [4, 4, 128, 14784], P('pp', 'dp', None, 'tp'), may hold values from -8 to 8
- up_pre: bfloat16 [4, 4, 128, 14784], P('pp', 'dp', None, 'tp'), may hold values from -6 to 6
- hidden_grad: bfloat16 [4, 4, 128, 14784], P('pp', 'dp', None, 'tp'), may hold values from -0.59765625 to 0.59765625
- gate_weight: bfloat16 [4, 4096, 14784], P('pp', 'dp', 'tp'), may hold values from -0.09375 to 0.09375
Outputs:
- passed_grad: bfloat16 [4, 4, 128, 4096], P('pp', 'dp', 'tp')
- gate_weight_grad: bfloat16 [4, 4096, 14784], P('pp', 'dp', 'tp')
All inputs are finite; a program needn't handle non-finite values.
Results may differ from a plain program's by a relative error of at most 0.018.
Values may be sent and summed in bfloat16 or wider, within the bound.
A program may use at most 64 MiB of HBM per device.

v0:
```python
import jax
import jax.numpy as jnp
from jax import lax
from jax.sharding import PartitionSpec as P


def cut_along(x, dim, peers):
    before, after = (x.shape[:dim], x.shape[dim + 1 :])
    return jnp.moveaxis(x.reshape(*before, peers, -1, *after), dim, 0)


def sent_and_summed(x, axis, dim):
    tiles = cut_along(x, dim, lax.axis_size(axis))
    arrived = lax.all_to_all(tiles, axis, split_axis=0, concat_axis=0, tiled=True)
    return arrived.astype(jnp.float32).sum(axis=0)


def from_everyone(x, axis):
    copies = jnp.broadcast_to(x, (lax.axis_size(axis), *x.shape))
    return lax.all_to_all(copies, axis, split_axis=0, concat_axis=0, tiled=True)


def laid_out(tiles, dim):
    tiles = jnp.moveaxis(tiles, 0, dim)
    lengths = tiles.shape
    return tiles.reshape(*lengths[:dim], lengths[dim] * lengths[dim + 1], *lengths[dim + 2 :])


def collect(x, axis, dim):
    tiles = from_everyone(x, axis)
    return laid_out(tiles, dim)


def from_behind(block, axis, distance):
    devices = range(lax.axis_size(axis))
    route = [(i - distance, i) for i in devices if i - distance in devices]
    return lax.ppermute(block, axis, route)


def finish(partial_value):
    return sent_and_summed(partial_value.astype(jnp.bfloat16), "tp", 0).astype(jnp.bfloat16)


def on_device(layer_input, gate_pre, up_pre, hidden_grad, gate_weight):
    tokens_in = layer_input[0, 0]
    gate_val = gate_pre[0, 0].astype(jnp.float32)
    up_val = up_pre[0, 0].astype(jnp.float32)
    hidden_val = hidden_grad[0, 0].astype(jnp.float32)
    gate_local = gate_weight[0]
    rows_total = gate_val.shape[0]
    groups = lax.axis_size("dp")
    logistic = jax.nn.sigmoid(gate_val)
    gate_grad = (hidden_val * up_val * logistic * (1.0 + gate_val * (1.0 - logistic))).astype(
        jnp.bfloat16
    )
    gathered_in = collect(tokens_in, "tp", 0)
    contract_cols = (((1,), (1,)), ((), ()))
    all_grads = collect(gate_grad, "dp", 0)
    partial_value = lax.dot_general(
        all_grads, gate_local, contract_cols, preferred_element_type=jnp.float32
    )
    returned = lax.all_to_all(
        partial_value.astype(jnp.bfloat16), "dp", split_axis=0, concat_axis=1, tiled=True
    ).astype(partial_value.dtype)
    input_grad = finish(returned)
    in_columns = lax.all_to_all(gathered_in, "dp", split_axis=1, concat_axis=0, tiled=True)
    products = lax.dot_general(
        in_columns.reshape(groups, rows_total, in_columns.shape[1]),
        all_grads.reshape(groups, rows_total, all_grads.shape[1]),
        (((1,), (1,)), ((0,), (0,))),
        preferred_element_type=jnp.float32,
    )
    rounded = lax.optimization_barrier(products.astype(jnp.bfloat16))
    grads_total = jnp.sum(rounded.astype(jnp.float32), axis=0)
    passed = from_behind(input_grad, "pp", -1)
    gate_out = grads_total.astype(jnp.bfloat16)
    return (passed[None, None], gate_out[None])


def solution(mesh):
    return jax.shard_map(
        on_device,
        mesh=mesh,
        in_specs=(
            P("pp", "dp", "tp", None),
            P("pp", "dp", None, "tp"),
            P("pp", "dp", None, "tp"),
            P("pp", "dp", None, "tp"),
            P("pp", "dp", "tp"),
        ),
        out_specs=(P("pp", "dp", "tp", None), P("pp", "dp", "tp")),
        check_vma=False,
    )
```

profile of v0, /device:TPU:96, one launch (start us, length us, event | category | flops | bytes accessed | tf_op | source)
XLA Modules:
  0.0 136.5 jit_solution(6257464139573123061)
XLA Ops:
  0.6 0.0 copy-start
  0.6 1.5 %fusion.11 = bf16[128,924]{0,1:T(8,128)(2,1)S(1)} fusion(bf16[1,1,128,924]{2,3,1,0:T(8,128)(2,1)} %param.7, bf16[1,1,128,924]{2,3,1,0:T(8,128)(2,1)} %param.8, bf16[1,1,128,924]{2,3,1,0:T(8,128)(2,1)} %param.6), kind=kLoop, calls=%fused_computation.13 | loop fusion | flops 1537536 | bytes 946176 | tf_op jit(solution)/shard_map/convert_element_type | solution.py:53
  2.2 0.1 broadcast_in_dim.12
  2.3 18.3 %all_to_all.47 = bf16[4,128,924]{1,2,0:T(8,128)(2,1)S(1)} all-to-all(bf16[4,128,924]{1,2,0:T(8,128)(2,1)S(1)} %broadcast_in_dim.12), channel_id=1, replica_groups=mesh['pp'=4,'tp'=16,'dp'=4] {'dp'}, dimensions={0} | all-to-all | bytes 1892352 | tf_op jit(solution)/shard_map/all_to_all | solution.py:20
  20.6 0.5 copy.15
  21.1 0.4 pad
  21.5 0.2 copy.13
  21.7 0.0 copy-done
  21.7 1.3 fusion.2
  23.0 0.0 copy-start.1
  23.0 17.2 %all_to_all.48 = bf16[4,128,1024]{2,1,0:T(8,128)(2,1)} all-to-all(bf16[4,128,1024]{2,1,0:T(8,128)(2,1)S(1)} %bitcast.35), channel_id=1, replica_groups=mesh['pp'=4,'tp'=16,'dp'=4] {'dp'}, dimensions={0} | all-to-all | bytes 2097152 | tf_op jit(solution)/shard_map/all_to_all | solution.py:62
  40.2 0.0 copy-done.1
  40.2 1.1 broadcast_in_dim.14
  41.3 8.6 %all-to-all-start.3 = ((bf16[16,8,4096]{2,1,0:T(8,128)(2,1)}), bf16[16,8,4096]{2,1,0:T(8,128)(2,1)}, u32[]{:S(2)}, u32[]{:S(2)}) async-start(bf16[16,8,4096]{2,1,0:T(8,128)(2,1)} %broadcast_in_dim.14), calls=%async_computation.3 | async-start | bytes 2097152 | tf_op jit(solution)/shard_map/all_to_all | solution.py:20
  49.9 3.0 %copy.11 = bf16[128,4,1024]{2,1,0:T(4,128)(2,1)} copy(bf16[128,4,1024]{2,0,1:T(8,128)(2,1)} %bitcast.31) | data formatting | bytes 2097152 | tf_op jit(solution)/shard_map/all_to_all | solution.py:62
  52.9 2.6 %reshape.27 = bf16[16,8,4096]{2,1,0:T(8,128)(2,1)} reshape(bf16[128,4,1024]{2,1,0:T(4,128)(2,1)} %copy.11) | data formatting | bytes 2097152 | tf_op jit(solution)/shard_map/reshape | solution.py:9
  55.5 18.3 %all-to-all-done.3 = bf16[16,8,4096]{2,1,0:T(8,128)(2,1)} async-done(((bf16[16,8,4096]{2,1,0:T(8,128)(2,1)}), bf16[16,8,4096]{2,1,0:T(8,128)(2,1)}, u32[]{:S(2)}, u32[]{:S(2)}) %all-to-all-start.3) | async-done | bytes 1048608 | tf_op jit(solution)/shard_map/all_to_all | solution.py:20
  73.8 6.0 %all-to-all-start.2 = ((bf16[16,8,4096]{2,1,0:T(8,128)(2,1)}), bf16[16,8,4096]{2,1,0:T(8,128)(2,1)}, u32[]{:S(2)}, u32[]{:S(2)}) async-start(bf16[16,8,4096]{2,1,0:T(8,128)(2,1)} %reshape.27), calls=%async_computation.2 | async-start | bytes 2097152 | tf_op jit(solution)/shard_map/all_to_all | solution.py:14
  79.8 2.6 %all_to_all.39 = bf16[128,4,1024]{2,1,0:T(4,128)(2,1)} reshape(bf16[16,8,4096]{2,1,0:T(8,128)(2,1)} %all-to-all-done.3) | data formatting | bytes 2097152 | tf_op jit(solution)/shard_map/all_to_all | solution.py:66
  82.4 2.6 %copy.12 = bf16[128,4,1024]{2,0,1:T(8,128)(2,1)} copy(bf16[128,4,1024]{2,1,0:T(4,128)(2,1)} %all_to_all.39) | data formatting | bytes 2097152 | tf_op jit(solution)/shard_map/all_to_all | solution.py:66
  85.0 19.1 %all-to-all-done.2 = bf16[16,8,4096]{2,1,0:T(8,128)(2,1)} async-done(((bf16[16,8,4096]{2,1,0:T(8,128)(2,1)}), bf16[16,8,4096]{2,1,0:T(8,128)(2,1)}, u32[]{:S(2)}, u32[]{:S(2)}) %all-to-all-start.2) | async-done | bytes 1048608 | tf_op jit(solution)/shard_map/all_to_all | solution.py:14
  104.1 4.2 %all-to-all-start.4 = ((bf16[128,4,1024]{2,0,1:T(8,128)(2,1)}), bf16[128,4,1024]{2,0,1:T(8,128)(2,1)}, u32[]{:S(2)}, u32[]{:S(2)}) async-start(bf16[128,4,1024]{2,0,1:T(8,128)(2,1)} %copy.12), calls=%async_computation.4 | async-start | bytes 2097152 | tf_op jit(solution)/shard_map/all_to_all | solution.py:66
  108.3 1.4 %reduce_sum.24 = bf16[8,4096]{1,0:T(8,128)(2,1)S(1)} reduce(bf16[16,8,4096]{2,1,0:T(8,128)(2,1)} %all-to-all-done.2, bf16[]{:T(256)} %constant.5.clone.1), dimensions={0}, to_apply=%region_0.0 | reduce | flops 491520 | bytes 1114114 | tf_op jit(solution)/shard_map/reduce_sum | solution.py:15
  109.7 1.3 collective-permute-start
  111.0 11.7 %all-to-all-done.4 = bf16[128,4,1024]{2,0,1:T(8,128)(2,1)} async-done(((bf16[128,4,1024]{2,0,1:T(8,128)(2,1)}), bf16[128,4,1024]{2,0,1:T(8,128)(2,1)}, u32[]{:S(2)}, u32[]{:S(2)}) %all-to-all-start.4) | async-done | bytes 1048608 | tf_op jit(solution)/shard_map/all_to_all | solution.py:66
  122.6 6.4 %convert_bitcast_fusion = bf16[4,1024,924]{1,2,0:T(8,128)(2,1)} fusion(bf16[4,128,924]{1,2,0:T(8,128)(2,1)S(1)} %all_to_all.47, bf16[128,4,1024]{2,0,1:T(8,128)(2,1)} %all-to-all-done.4), kind=kOutput, calls=%fused_computation | convolution fusion | flops 972668928 | bytes 9564160 | tf_op jit(solution)/shard_map/dot_general | solution.py:67
  129.0 6.9 %reduce_sum.25 = bf16[1024,924]{0,1:T(8,128)(2,1)} reduce(bf16[4,1024,924]{1,2,0:T(8,128)(2,1)} %convert_bitcast_fusion, bf16[]{:T(256)} %constant.5.clone.1), dimensions={0}, to_apply=%region_1.0 | reduce | flops 2838528 | bytes 9461762 | tf_op jit(solution)/shard_map/reduce_sum | solution.py:74
  135.9 0.0 collective-permute-done
  135.9 0.6 copy.17
Async XLA Ops:
  0.6 21.0 %copy-start = (bf16[1,1024,924]{1,2,0:T(8,128)(2,1)S(1)}, bf16[1,1024,924]{1,2,0:T(8,128)(2,1)}, u32[]{:S(2)}) copy-start(bf16[1,1024,924]{1,2,0:T(8,128)(2,1)} %param.9) | copy-start | bytes 5677060
  23.0 17.3 %copy-start.1 = (bf16[1,1,8,4096]{3,2,1,0:T(8,128)(2,1)S(1)}, bf16[1,1,8,4096]{3,2,1,0:T(8,128)(2,1)}, u32[]{:S(2)}) copy-start(bf16[1,1,8,4096]{3,2,1,0:T(8,128)(2,1)} %param.5) | copy-start | bytes 196612
  41.3 32.5 %all-to-all-start.3 = ((bf16[16,8,4096]{2,1,0:T(8,128)(2,1)}), bf16[16,8,4096]{2,1,0:T(8,128)(2,1)}, u32[]{:S(2)}, u32[]{:S(2)}) async-start(bf16[16,8,4096]{2,1,0:T(8,128)(2,1)} %broadcast_in_dim.14), calls=%async_computation.3 | async-start | bytes 2097152 | tf_op jit(solution)/shard_map/all_to_all | solution.py:20
  73.8 30.3 %all-to-all-start.2 = ((bf16[16,8,4096]{2,1,0:T(8,128)(2,1)}), bf16[16,8,4096]{2,1,0:T(8,128)(2,1)}, u32[]{:S(2)}, u32[]{:S(2)}) async-start(bf16[16,8,4096]{2,1,0:T(8,128)(2,1)} %reshape.27), calls=%async_computation.2 | async-start | bytes 2097152 | tf_op jit(solution)/shard_map/all_to_all | solution.py:14
  104.1 18.6 %all-to-all-start.4 = ((bf16[128,4,1024]{2,0,1:T(8,128)(2,1)}), bf16[128,4,1024]{2,0,1:T(8,128)(2,1)}, u32[]{:S(2)}, u32[]{:S(2)}) async-start(bf16[128,4,1024]{2,0,1:T(8,128)(2,1)} %copy.12), calls=%async_computation.4 | async-start | bytes 2097152 | tf_op jit(solution)/shard_map/all_to_all | solution.py:66
  109.7 26.2 %collective-permute-start = (bf16[8,4096]{1,0:T(8,128)(2,1)S(1)}, bf16[8,4096]{1,0:T(8,128)(2,1)S(1)}, u32[]{:S(2)}, u32[]{:S(2)}) collective-permute-start(bf16[8,4096]{1,0:T(8,128)(2,1)S(1)} %reduce_sum.24), channel_id=1, source_target_pairs={{64,0},{128,64},{192,128},{65,1},{129,65},{193,129},{66,2},{130,66... | collective-permute-start | bytes 196616 | tf_op jit(solution)/shard_map/ppermute | solution.py:37
where the time goes:
time: 137 us
  waiting for transfers between devices  49 us (36%)
  blocking collectives  35.5 us (26%)
  starting transfers between devices  20.1 us (15%)
  local copies, waits for them, and re-layouts  13.7 us (10%)
  other arithmetic  9.78 us (7%)
  matrix products  7.67 us (6%)
    all_to_all x1, waiting for transfers between devices, sent_and_summed(): lax.all_to_all(tiles, axis, split_axis=0, concat_axis=0, tiled=True)  19.1 us
    all_to_all x1, blocking collectives, from_everyone(): return lax.all_to_all(copies, axis, split_axis=0, concat_axis=0, tiled=True)  18.3 us
    all_to_all x1, waiting for transfers between devices, from_everyone(): return lax.all_to_all(copies, axis, split_axis=0, concat_axis=0, tiled=True)  18.3 us
    all_to_all x1, blocking collectives, on_device(): lax.all_to_all(partial_value.astype(jnp.bfloat16), 'dp', split_axis=0, co...  17.2 us
    all_to_all x1, waiting for transfers between devices, on_device(): lax.all_to_all(gathered_in, 'dp', split_axis=1, concat_axis=0, tiled=True)  11.7 us
    all_to_all x1, starting transfers between devices, from_everyone(): return lax.all_to_all(copies, axis, split_axis=0, concat_axis=0, tiled=True)  8.6 us
    reduce_sum x1, other arithmetic, on_device(): grads_total = jnp.sum(rounded.astype(jnp.float32), axis=0)  6.88 us
    dot_general x1, matrix products, on_device(): lax.dot_general(in_columns.reshape(groups, rows_total, in_columns.shape[1...  6.38 us
  transfers between devices with their start and end apart: 4, of which 3 were waited for; matrix products, arithmetic and copies ran while one was open for 17% of the time, Pallas kernels for 0%

commit v1 on v0

v1 whole, which is shorter than its diff:
```python
import jax
import jax.numpy as jnp
from jax import lax
from jax.experimental import pallas as pl
from jax.experimental.pallas import tpu as pltpu
from jax.sharding import PartitionSpec as P

MESH = pl.DeviceIdType.MESH
F32 = jnp.float32
BF16 = jnp.bfloat16


def kernel(
    x_hbm, gate_hbm, up_hbm, hid_hbm, w_hbm,
    dx_ref, dw_ref,
    gate_v, up_v, hid_v, w_v, g_all, x_all, x_mat, part, ring, fin, landed,
    load_sem, xs, xr, ps, pr, gs, gr, ags, agr, rss, rsr, fs, fr,
):
    p, t, y = lax.axis_index("pp"), lax.axis_index("tp"), lax.axis_index("dp")
    n_pp, n_dp = lax.axis_size("pp"), lax.axis_size("dp")
    z, xl = t // 2, lax.rem(t, 2)
    nz = 8
    hidden = gate_hbm.shape[0]
    half = g_all.shape[2]
    rest = hidden - half
    cols = w_hbm.shape[1]
    hc = cols // 2

    def zmod(v):
        return lax.rem(v + 2 * nz, nz)

    def ymod(v):
        return lax.rem(v + 2 * n_dp, n_dp)

    def at_z(d):
        return (p, zmod(z + d) * 2 + xl, y)

    def at_y(d):
        return (p, t, ymod(y + d))

    partner = (p, t + 1 - 2 * xl, y)

    def remote(src, dst, ssem, rsem, dev):
        return pltpu.make_async_remote_copy(
            src_ref=src, dst_ref=dst, send_sem=ssem, recv_sem=rsem,
            device_id=dev, device_id_type=MESH,
        )

    loads = [
        pltpu.make_async_copy(gate_hbm, gate_v, load_sem.at[0]),
        pltpu.make_async_copy(up_hbm, up_v, load_sem.at[1]),
        pltpu.make_async_copy(hid_hbm, hid_v, load_sem.at[2]),
        pltpu.make_async_copy(w_hbm, w_v, load_sem.at[3]),
        pltpu.make_async_copy(
            x_hbm.at[:, pl.ds(pl.multiple_of(y * cols, 128), cols)],
            x_all.at[z, xl, y], load_sem.at[4]),
    ]
    for c in loads:
        c.start()

    barrier = pltpu.get_barrier_semaphore()
    peers = [at_y(1), at_y(2), at_y(3), at_z(1), at_z(-1), partner]
    for d in peers:
        pl.semaphore_signal(barrier, inc=1, device_id=d, device_id_type=MESH)

    @pl.when(p < n_pp - 1)
    def _():
        for j in range(4):
            for xq in range(2):
                pl.semaphore_signal(
                    barrier, inc=1, device_id=(p + 1, z * 2 + xq, j), device_id_type=MESH)

    pl.semaphore_wait(barrier, jnp.where(p > 0, len(peers) + 8, len(peers)))

    sends = []

    def go(c):
        c.start()
        sends.append(c)

    def x_copy(k):
        j = ymod(y + k)
        return remote(
            x_hbm.at[:, pl.ds(pl.multiple_of(j * cols, 128), cols)],
            x_all.at[z, xl, y], xs.at[k - 1], xr.at[k - 1], at_y(k))

    for k in (1, 3, 2):
        go(x_copy(k))

    for c in loads[:3]:
        c.wait()
    for h, (lo, n) in enumerate(((0, half), (half, rest))):
        rows = pl.ds(lo, n)
        g = gate_v[rows, :].astype(F32)
        u = up_v[rows, :].astype(F32)
        d = hid_v[rows, :].astype(F32)
        s = jax.nn.sigmoid(g)
        v = d * u * s * (1.0 + g * (1.0 - s))
        if n < half:
            v = jnp.concatenate([v, jnp.zeros((half - n, v.shape[1]), F32)], axis=0)
        g_all[y, h] = v.astype(BF16)

    def g_copy(plus, k):
        if plus:
            owner, h, dev = ((y, 0), (y, 1), (ymod(y - 1), 0))[k] + (at_y(1),)
        else:
            owner, h, dev = ((y, 1), (y, 0), (ymod(y + 1), 1))[k] + (at_y(-1),)
        i = 0 if plus else 1
        ref = g_all.at[owner, h]
        return remote(ref, ref, gs.at[i, k], gr.at[i, k], dev)

    for k in (0, 1):
        go(g_copy(True, k))
        go(g_copy(False, k))

    def rep(ri):
        return ymod(y + (0, 1, 3, 2)[ri])

    def product(ri):
        r = rep(ri)
        g = jnp.concatenate([g_all[r, 0], g_all[r, 1]], axis=0)[:hidden]
        for q in range(2):
            c = pl.ds(q * hc, hc)
            acc = lax.dot_general(
                g, w_v[:, c], (((0,), (0,)), ((), ())), preferred_element_type=F32)
            part[ri, :, :, c] = acc.astype(BF16).reshape(nz, 16, hc)

    def lanes(plus):
        return pl.ds(0, hc) if plus else pl.ds(hc, hc)

    def rs_copy(plus, ri, s):
        i, sign = (0, 1) if plus else (1, -1)
        src = part.at[ri, zmod(z + sign * (5 - s))]
        dst = ring.at[i, ri, s - 1]
        if s == 1:
            src, dst = src.at[:, lanes(plus)], dst.at[:, lanes(plus)]
        return remote(src, dst, rss.at[i, ri, s - 1], rsr.at[i, ri, s - 1], at_z(sign))

    def rs_start(ri):
        for plus in (True, False):
            go(rs_copy(plus, ri, 1))

    def rs_next(ri, s):
        for plus in (True, False):
            i, sign = (0, 1) if plus else (1, -1)
            rs_copy(plus, ri, s - 1).wait_recv()
            d = zmod(z + sign * (5 - s))
            c = lanes(plus) if s == 2 else pl.ds(0, cols)
            part[ri, d, :, c] = (
                part[ri, d, :, c].astype(F32) + ring[i, ri, s - 2, :, c].astype(F32)
            ).astype(BF16)
            go(rs_copy(plus, ri, s))

    def fin_copy(ri, xq):
        return remote(
            fin.at[ri, xq], landed.at[y, xl], fs.at[ri, xq], fr.at[y, xl],
            (jnp.maximum(p - 1, 0), z * 2 + xq, rep(ri)))

    def rs_end(ri):
        for plus in (True, False):
            rs_copy(plus, ri, 4).wait_recv()
        v = (
            part[ri, z].astype(F32) + ring[0, ri, 3].astype(F32) + ring[1, ri, 3].astype(F32)
        )
        v = v.reshape(2, 8, cols).astype(BF16)
        for xq in range(2):
            fin[ri, xq] = v[xq]

        @pl.when(p > 0)
        def _():
            for xq in range(2):
                fin_copy(ri, xq).start()

    def pair_copy():
        ref = x_all.at[z, xl]
        return remote(ref, ref, ps.at[0], pr.at[0], partner)

    def ag_copy(plus, slot, s):
        i, sign = (0, 1) if plus else (1, -1)
        col = xl if slot == 0 else 1 - xl
        ref = x_all.at[zmod(z - sign * (s - 1)), col]
        if s == 4:
            ref = ref.at[pl.ds(0, 2)] if plus else ref.at[pl.ds(2, 2)]
        return remote(
            ref, ref, ags.at[i, slot, s - 1], agr.at[i, slot, s - 1], at_z(sign))

    def ag_start(slot):
        for plus in (True, False):
            go(ag_copy(plus, slot, 1))

    def ag_next(slot, s):
        for plus in (True, False):
            ag_copy(plus, slot, s - 1).wait_recv()
            go(ag_copy(plus, slot, s))

    def ag_end(slot):
        for plus in (True, False):
            ag_copy(plus, slot, 4).wait_recv()

    loads[3].wait()
    product(0)
    rs_start(0)

    loads[4].wait()
    for k in (1, 3, 2):
        x_copy(k).wait_recv()
    go(pair_copy())
    ag_start(0)

    g_copy(True, 0).wait_recv()
    go(g_copy(True, 2))
    g_copy(False, 0).wait_recv()
    go(g_copy(False, 2))

    rs_next(0, 2)
    pair_copy().wait_recv()
    ag_start(1)
    ag_next(0, 2)

    g_copy(True, 1).wait_recv()
    g_copy(False, 1).wait_recv()
    product(1)
    rs_start(1)
    product(2)
    rs_start(2)
    rs_next(0, 3)
    ag_next(1, 2)

    g_copy(True, 2).wait_recv()
    g_copy(False, 2).wait_recv()
    product(3)
    rs_start(3)
    rs_next(1, 2)
    rs_next(2, 2)
    rs_next(0, 4)
    ag_next(0, 3)
    rs_next(3, 2)
    rs_next(1, 3)
    rs_next(2, 3)
    rs_end(0)
    ag_next(1, 3)
    rs_next(3, 3)
    rs_next(1, 4)
    rs_next(2, 4)
    ag_next(0, 4)
    rs_next(3, 4)
    ag_next(1, 4)
    rs_end(1)
    rs_end(2)
    rs_end(3)

    ag_end(0)
    ag_end(1)
    for r in range(4):
        x_mat[pl.ds(r * 128, 128), :] = (
            x_all[:, :, r].astype(F32).reshape(128, cols).astype(BF16))
    for lo in range(0, hidden, 128):
        n = min(128, hidden - lo)
        pieces = []
        for r in range(4):
            if lo + n <= half:
                pieces.append(g_all[r, 0, pl.ds(lo, n), :])
            elif lo >= half:
                pieces.append(g_all[r, 1, pl.ds(lo - half, n), :])
            else:
                pieces.append(jnp.concatenate(
                    [g_all[r, 0, pl.ds(lo, half - lo), :],
                     g_all[r, 1, pl.ds(0, lo + n - half), :]], axis=0))
        g = jnp.concatenate(pieces, axis=1)
        dw_ref[pl.ds(lo, n), :] = jnp.dot(
            g, x_mat[...], preferred_element_type=F32).astype(BF16)

    @pl.when(p < n_pp - 1)
    def _():
        for j in range(4):
            for xq in range(2):
                remote(
                    landed.at[j, xq], landed.at[j, xq], fs.at[0, 0], fr.at[j, xq],
                    partner).wait_recv()
            dx_ref[:, pl.ds(j * cols, cols)] = (
                landed[j, 0].astype(F32) + landed[j, 1].astype(F32)).astype(BF16)

    @pl.when(p == n_pp - 1)
    def _():
        dx_ref[...] = jnp.zeros_like(dx_ref)

    for c in sends:
        c.wait_send()

    @pl.when(p > 0)
    def _():
        for ri in range(4):
            for xq in range(2):
                fin_copy(ri, xq).wait_send()


def on_device(layer_input, gate_pre, up_pre, hidden_grad, gate_weight):
    x = layer_input[0, 0]
    gate, up, hid = (jnp.swapaxes(v[0, 0], 0, 1) for v in (gate_pre, up_pre, hidden_grad))
    w = jnp.swapaxes(gate_weight[0], 0, 1)
    hidden, toks = gate.shape
    cols = w.shape[1]
    half = (hidden // 2 + 15) // 16 * 16
    vm = pltpu.VMEM
    dma = pltpu.SemaphoreType.DMA
    dx, dw = pl.pallas_call(
        kernel,
        name="section",
        out_shape=(
            jax.ShapeDtypeStruct(x.shape, BF16),
            jax.ShapeDtypeStruct((hidden, cols), BF16),
        ),
        in_specs=[pl.BlockSpec(memory_space=pl.ANY)] * 5,
        out_specs=[pl.BlockSpec(memory_space=pltpu.VMEM)] * 2,
        scratch_shapes=[
            vm((hidden, toks), BF16), vm((hidden, toks), BF16), vm((hidden, toks), BF16),
            vm((hidden, cols), BF16),
            vm((4, 2, half, toks), BF16),
            vm((8, 2, 4, 8, cols), BF16),
            vm((512, cols), BF16),
            vm((4, 8, 16, cols), BF16),
            vm((2, 4, 4, 16, cols), BF16),
            vm((4, 2, 8, cols), BF16),
            vm((4, 2, 8, cols), BF16),
            dma((5,)), dma((3,)), dma((3,)), dma((1,)), dma((1,)),
            dma((2, 3)), dma((2, 3)),
            dma((2, 2, 4)), dma((2, 2, 4)),
            dma((2, 4, 4)), dma((2, 4, 4)),
            dma((4, 2)), dma((4, 2)),
        ],
        compiler_params=pltpu.CompilerParams(
            collective_id=0, has_side_effects=True, vmem_limit_bytes=40 << 20),
    )(x, gate, up, hid, w)
    return dx[None, None], jnp.swapaxes(dw, 0, 1)[None]


def solution(mesh):
    return jax.shard_map(
        on_device,
        mesh=mesh,
        in_specs=(
            P("pp", "dp", "tp", None),
            P("pp", "dp", None, "tp"),
            P("pp", "dp", None, "tp"),
            P("pp", "dp", None, "tp"),
            P("pp", "dp", "tp"),
        ),
        out_specs=(P("pp", "dp", "tp", None), P("pp", "dp", "tp")),
        check_vma=False,
    )
```

time: 137 us -> 51.6 us (0.38)
  the two profiles are of different devices: /device:TPU:96 before, /device:TPU:1 now
where the time goes in v1:
time: 51.6 us; the launch traced here: 51.4 us
  Pallas kernels  43.6 us (84%)
  local copies, waits for them, and re-layouts  7.06 us (14%)
  between operations  0.65 us (1%)
    pallas_call x1, Pallas kernels, on_device(): pl.pallas_call(kernel, name='section', out_shape=(jax.ShapeDtypeStruct(x....  43.6 us
    unnamed x12, local copies, waits for them, and re-layouts  7.06 us

profile of v1, /device:TPU:1, one launch (start us, length us, event | category | flops | bytes accessed | tf_op | source)
XLA Modules:
  0.0 51.4 jit_solution(8236247452689970854)
XLA Ops:
  0.6 0.0 copy-start
  0.6 1.5 %copy-done = bf16[1,1024,924]{1,2,0:T(8,128)(2,1)S(1)} copy-done((bf16[1,1024,924]{1,2,0:T(8,128)(2,1)S(1)}, bf16[1,1024,924]{1,2,0:T(8,128)(2,1)}, u32[]{:S(2)}) %copy-start) | copy-done | bytes 1892376
  2.2 0.0 copy-start.1
  2.2 0.9 %copy-done.1 = bf16[1,1,128,924]{2,3,1,0:T(8,128)(2,1)S(1)} copy-done((bf16[1,1,128,924]{2,3,1,0:T(8,128)(2,1)S(1)}, bf16[1,1,128,924]{2,3,1,0:T(8,128)(2,1)}, u32[]{:S(2)}) %copy-start.1) | copy-done | bytes 236568
  3.1 0.0 copy-start.2
  3.1 0.9 %copy-done.2 = bf16[1,1,128,924]{2,3,1,0:T(8,128)(2,1)S(1)} copy-done((bf16[1,1,128,924]{2,3,1,0:T(8,128)(2,1)S(1)}, bf16[1,1,128,924]{2,3,1,0:T(8,128)(2,1)}, u32[]{:S(2)}) %copy-start.2) | copy-done | bytes 236568
  4.0 0.0 copy-start.3
  4.0 0.9 %copy-done.3 = bf16[1,1,128,924]{2,3,1,0:T(8,128)(2,1)S(1)} copy-done((bf16[1,1,128,924]{2,3,1,0:T(8,128)(2,1)S(1)}, bf16[1,1,128,924]{2,3,1,0:T(8,128)(2,1)}, u32[]{:S(2)}) %copy-start.3) | copy-done | bytes 236568
  5.0 0.0 copy-start.4
  5.0 0.8 %copy-done.4 = bf16[1,1,8,4096]{3,2,1,0:T(8,128)(2,1)S(1)} copy-done((bf16[1,1,8,4096]{3,2,1,0:T(8,128)(2,1)S(1)}, bf16[1,1,8,4096]{3,2,1,0:T(8,128)(2,1)}, u32[]{:S(2)}) %copy-start.4) | copy-done | bytes 65560
  5.8 43.6 %section.1 = (bf16[8,4096]{1,0:T(8,128)(2,1)S(1)}, bf16[924,1024]{1,0:T(8,128)(2,1)S(1)}) custom-call(bf16[8,4096]{1,0:T(8,128)(2,1)S(1)} %bitcast.23, bf16[924,128]{1,0:T(8,128)(2,1)S(1)} %bitcast.19, bf16[924,128]{1,0:T(8,128)(2,1)S(1)} %bitcast.20, bf16[924,128]{1,0:T(8,128)(2,1)S(1)} %bitcast.21, bf16[924,1024]{1,0:T(8,128)(2,1)S(1)} %bitcast.17), custom_call_target="tpu_custom_call" | custom-call | tf_op jit(solution)/shard_map/section/pallas_call | solution.py:306
  49.5 0.6 %copy.9 = bf16[1,1,8,4096]{3,2,1,0:T(8,128)(2,1)} copy(bf16[1,1,8,4096]{3,2,1,0:T(8,128)(2,1)S(1)} %bitcast.22) | data formatting | bytes 131072
  50.1 1.2 %copy.10 = bf16[1,1024,924]{1,2,0:T(8,128)(2,1)} copy(bf16[1,1024,924]{1,2,0:T(8,128)(2,1)S(1)} %bitcast.18) | data formatting | bytes 3784704
Async XLA Ops:
  0.6 1.5 %copy-start = (bf16[1,1024,924]{1,2,0:T(8,128)(2,1)S(1)}, bf16[1,1024,924]{1,2,0:T(8,128)(2,1)}, u32[]{:S(2)}) copy-start(bf16[1,1024,924]{1,2,0:T(8,128)(2,1)} %param.9) | copy-start | bytes 5677060
  2.2 0.9 %copy-start.1 = (bf16[1,1,128,924]{2,3,1,0:T(8,128)(2,1)S(1)}, bf16[1,1,128,924]{2,3,1,0:T(8,128)(2,1)}, u32[]{:S(2)}) copy-start(bf16[1,1,128,924]{2,3,1,0:T(8,128)(2,1)} %param.6) | copy-start | bytes 709636
  3.1 0.9 %copy-start.2 = (bf16[1,1,128,924]{2,3,1,0:T(8,128)(2,1)S(1)}, bf16[1,1,128,924]{2,3,1,0:T(8,128)(2,1)}, u32[]{:S(2)}) copy-start(bf16[1,1,128,924]{2,3,1,0:T(8,128)(2,1)} %param.7) | copy-start | bytes 709636
  4.0 0.9 %copy-start.3 = (bf16[1,1,128,924]{2,3,1,0:T(8,128)(2,1)S(1)}, bf16[1,1,128,924]{2,3,1,0:T(8,128)(2,1)}, u32[]{:S(2)}) copy-start(bf16[1,1,128,924]{2,3,1,0:T(8,128)(2,1)} %param.8) | copy-start | bytes 709636
  5.0 0.8 %copy-start.4 = (bf16[1,1,8,4096]{3,2,1,0:T(8,128)(2,1)S(1)}, bf16[1,1,8,4096]{3,2,1,0:T(8,128)(2,1)}, u32[]{:S(2)}) copy-start(bf16[1,1,8,4096]{3,2,1,0:T(8,128)(2,1)} %param.5) | copy-start | bytes 196612

commit v2 on v1

--- a/solution.py
+++ b/solution.py
@@ -13,7 +13,7 @@
 def kernel(
     x_hbm, gate_hbm, up_hbm, hid_hbm, w_hbm,
     dx_ref, dw_ref,
-    gate_v, up_v, hid_v, w_v, g_all, x_all, x_mat, part, ring, fin, landed,
+    gate_v, up_v, hid_v, w_v, x_v, g_all, x_all, x_mat, part, ring, fin, landed,
     load_sem, xs, xr, ps, pr, gs, gr, ags, agr, rss, rsr, fs, fr,
 ):
     p, t, y = lax.axis_index("pp"), lax.axis_index("tp"), lax.axis_index("dp")
@@ -54,12 +54,13 @@
         pltpu.make_async_copy(
             x_hbm.at[:, pl.ds(pl.multiple_of(y * cols, 128), cols)],
             x_all.at[z, xl, y], load_sem.at[4]),
+        pltpu.make_async_copy(x_hbm, x_v, load_sem.at[5]),
     ]
-    for c in loads:
-        c.start()
+    for i in (5, 0, 1, 2, 4, 3):
+        loads[i].start()
 
     barrier = pltpu.get_barrier_semaphore()
-    peers = [at_y(1), at_y(2), at_y(3), at_z(1), at_z(-1), partner]
+    peers = [at_y(1), at_y(2), at_y(3), at_z(1), at_z(-1), at_z(2), at_z(-2), partner]
     for d in peers:
         pl.semaphore_signal(barrier, inc=1, device_id=d, device_id_type=MESH)
 
@@ -81,10 +82,11 @@
     def x_copy(k):
         j = ymod(y + k)
         return remote(
-            x_hbm.at[:, pl.ds(pl.multiple_of(j * cols, 128), cols)],
+            x_v.at[:, pl.ds(pl.multiple_of(j * cols, 128), cols)],
             x_all.at[z, xl, y], xs.at[k - 1], xr.at[k - 1], at_y(k))
 
-    for k in (1, 3, 2):
+    loads[5].wait()
+    for k in (2, 1, 3):
         go(x_copy(k))
 
     for c in loads[:3]:
@@ -128,28 +130,33 @@
     def lanes(plus):
         return pl.ds(0, hc) if plus else pl.ds(hc, hc)
 
-    def rs_copy(plus, ri, s):
+    def rs_copy(plus, ri, kind):
         i, sign = (0, 1) if plus else (1, -1)
-        src = part.at[ri, zmod(z + sign * (5 - s))]
-        dst = ring.at[i, ri, s - 1]
-        if s == 1:
+        dest, hop = ((3, 1), (4, 2), (1, 1), (2, 2))[kind]
+        src = part.at[ri, zmod(z + sign * dest)]
+        dst = ring.at[i, ri, kind]
+        if kind == 1:
             src, dst = src.at[:, lanes(plus)], dst.at[:, lanes(plus)]
-        return remote(src, dst, rss.at[i, ri, s - 1], rsr.at[i, ri, s - 1], at_z(sign))
-
-    def rs_start(ri):
-        for plus in (True, False):
-            go(rs_copy(plus, ri, 1))
-
-    def rs_next(ri, s):
+        return remote(src, dst, rss.at[i, ri, kind], rsr.at[i, ri, kind], at_z(sign * hop))
+
+    def rs_send(ri, *kinds):
+        for kind in kinds:
+            for plus in (True, False):
+                go(rs_copy(plus, ri, kind))
+
+    def rs_mid(ri):
         for plus in (True, False):
             i, sign = (0, 1) if plus else (1, -1)
-            rs_copy(plus, ri, s - 1).wait_recv()
-            d = zmod(z + sign * (5 - s))
-            c = lanes(plus) if s == 2 else pl.ds(0, cols)
-            part[ri, d, :, c] = (
-                part[ri, d, :, c].astype(F32) + ring[i, ri, s - 2, :, c].astype(F32)
-            ).astype(BF16)
-            go(rs_copy(plus, ri, s))
+            for kind in (0, 1):
+                rs_copy(plus, ri, kind).wait_recv()
+            d = zmod(z + sign * 2)
+            for q in range(2):
+                c = pl.ds(q * hc, hc)
+                v = part[ri, d, :, c].astype(F32) + ring[i, ri, 0, :, c].astype(F32)
+                if plus == (q == 0):
+                    v = v + ring[i, ri, 1, :, c].astype(F32)
+                part[ri, d, :, c] = v.astype(BF16)
+            go(rs_copy(plus, ri, 3))
 
     def fin_copy(ri, xq):
         return remote(
@@ -157,11 +164,11 @@
             (jnp.maximum(p - 1, 0), z * 2 + xq, rep(ri)))
 
     def rs_end(ri):
-        for plus in (True, False):
-            rs_copy(plus, ri, 4).wait_recv()
-        v = (
-            part[ri, z].astype(F32) + ring[0, ri, 3].astype(F32) + ring[1, ri, 3].astype(F32)
-        )
+        v = part[ri, z].astype(F32)
+        for kind in (2, 3):
+            for plus in (True, False):
+                rs_copy(plus, ri, kind).wait_recv()
+                v = v + ring[0 if plus else 1, ri, kind].astype(F32)
         v = v.reshape(2, 8, cols).astype(BF16)
         for xq in range(2):
             fin[ri, xq] = v[xq]
@@ -171,86 +178,81 @@
             for xq in range(2):
                 fin_copy(ri, xq).start()
 
-    def pair_copy():
-        ref = x_all.at[z, xl]
-        return remote(ref, ref, ps.at[0], pr.at[0], partner)
-
-    def ag_copy(plus, slot, s):
+    def pair_copy(k):
+        ref = x_all.at[zmod(z + k), xl]
+        return remote(ref, ref, ps.at[k % nz], pr.at[k % nz], partner)
+
+    def ag_copy(plus, kind):
         i, sign = (0, 1) if plus else (1, -1)
-        col = xl if slot == 0 else 1 - xl
-        ref = x_all.at[zmod(z - sign * (s - 1)), col]
-        if s == 4:
+        origin, hop = ((0, 1), (0, 2), (-2, 1), (-2, 2))[kind]
+        ref = x_all.at[zmod(z + sign * origin), xl]
+        if kind == 3:
             ref = ref.at[pl.ds(0, 2)] if plus else ref.at[pl.ds(2, 2)]
-        return remote(
-            ref, ref, ags.at[i, slot, s - 1], agr.at[i, slot, s - 1], at_z(sign))
-
-    def ag_start(slot):
+        return remote(ref, ref, ags.at[i, kind], agr.at[i, kind], at_z(sign * hop))
+
+    def ag_send(*kinds):
+        for kind in kinds:
+            for plus in (True, False):
+                go(ag_copy(plus, kind))
+
+    def ag_wait(kind):
         for plus in (True, False):
-            go(ag_copy(plus, slot, 1))
-
-    def ag_next(slot, s):
-        for plus in (True, False):
-            ag_copy(plus, slot, s - 1).wait_recv()
-            go(ag_copy(plus, slot, s))
-
-    def ag_end(slot):
-        for plus in (True, False):
-            ag_copy(plus, slot, 4).wait_recv()
+            ag_copy(plus, kind).wait_recv()
 
     loads[3].wait()
     product(0)
-    rs_start(0)
+    rs_send(0, 1, 0)
 
     loads[4].wait()
     for k in (1, 3, 2):
         x_copy(k).wait_recv()
-    go(pair_copy())
-    ag_start(0)
-
+    ag_send(1, 0)
+    go(pair_copy(0))
+    rs_send(0, 2)
+
+    rs_mid(0)
     g_copy(True, 0).wait_recv()
     go(g_copy(True, 2))
     g_copy(False, 0).wait_recv()
     go(g_copy(False, 2))
 
-    rs_next(0, 2)
-    pair_copy().wait_recv()
-    ag_start(1)
-    ag_next(0, 2)
+    ag_wait(1)
+    ag_send(3, 2)
+    go(pair_copy(2))
+    go(pair_copy(-2))
 
     g_copy(True, 1).wait_recv()
     g_copy(False, 1).wait_recv()
     product(1)
-    rs_start(1)
+    rs_send(1, 1, 0)
     product(2)
-    rs_start(2)
-    rs_next(0, 3)
-    ag_next(1, 2)
+    rs_send(2, 1, 0)
+    ag_wait(0)
+    go(pair_copy(1))
+    go(pair_copy(-1))
+    rs_end(0)
 
     g_copy(True, 2).wait_recv()
     g_copy(False, 2).wait_recv()
     product(3)
-    rs_start(3)
-    rs_next(1, 2)
-    rs_next(2, 2)
-    rs_next(0, 4)
-    ag_next(0, 3)
-    rs_next(3, 2)
-    rs_next(1, 3)
-    rs_next(2, 3)
-    rs_end(0)
-    ag_next(1, 3)
-    rs_next(3, 3)
-    rs_next(1, 4)
-    rs_next(2, 4)
-    ag_next(0, 4)
-    rs_next(3, 4)
-    ag_next(1, 4)
+    rs_send(3, 1, 0)
+    rs_send(1, 2)
+    rs_send(2, 2)
+    rs_send(3, 2)
+    rs_mid(1)
+    rs_mid(2)
+    ag_wait(2)
+    go(pair_copy(3))
+    go(pair_copy(-3))
+    ag_wait(3)
+    go(pair_copy(4))
+    rs_mid(3)
     rs_end(1)
     rs_end(2)
     rs_end(3)
 
-    ag_end(0)
-    ag_end(1)
+    for k in range(nz):
+        pair_copy(k).wait_recv()
     for r in range(4):
         x_mat[pl.ds(r * 128, 128), :] = (
             x_all[:, :, r].astype(F32).reshape(128, cols).astype(BF16))
@@ -310,11 +312,12 @@
             jax.ShapeDtypeStruct(x.shape, BF16),
             jax.ShapeDtypeStruct((hidden, cols), BF16),
         ),
-        in_specs=[pl.BlockSpec(memory_space=pl.ANY)] * 5,
+        in_specs=[pl.BlockSpec(memory_space=pltpu.HBM)] * 5,
         out_specs=[pl.BlockSpec(memory_space=pltpu.VMEM)] * 2,
         scratch_shapes=[
             vm((hidden, toks), BF16), vm((hidden, toks), BF16), vm((hidden, toks), BF16),
             vm((hidden, cols), BF16),
+            vm(x.shape, BF16),
             vm((4, 2, half, toks), BF16),
             vm((8, 2, 4, 8, cols), BF16),
             vm((512, cols), BF16),
@@ -322,15 +325,15 @@
             vm((2, 4, 4, 16, cols), BF16),
             vm((4, 2, 8, cols), BF16),
             vm((4, 2, 8, cols), BF16),
-            dma((5,)), dma((3,)), dma((3,)), dma((1,)), dma((1,)),
+            dma((6,)), dma((3,)), dma((3,)), dma((8,)), dma((8,)),
             dma((2, 3)), dma((2, 3)),
-            dma((2, 2, 4)), dma((2, 2, 4)),
+            dma((2, 4)), dma((2, 4)),
             dma((2, 4, 4)), dma((2, 4, 4)),
             dma((4, 2)), dma((4, 2)),
         ],
         compiler_params=pltpu.CompilerParams(
             collective_id=0, has_side_effects=True, vmem_limit_bytes=40 << 20),
-    )(x, gate, up, hid, w)
+    )(*(pltpu.with_memory_space_constraint(v, pltpu.HBM) for v in (x, gate, up, hid, w)))
     return dx[None, None], jnp.swapaxes(dw, 0, 1)[None]
 
 

time: 51.6 us -> 44.2 us (0.86)
  local copies, waits for them, and re-layouts: 7.06 us -> 1.88 us
  Pallas kernels: 43.6 us -> 41.6 us
    unnamed x12 -> x2, local copies, waits for them, and re-layouts: 7.06 us -> 1.88 us
    pallas_call x1, Pallas kernels: 43.6 us -> 41.6 us  [on_device(): pl.pallas_call(kernel, name='section', out_shape=(jax.ShapeDtypeStruct(x....]
where the time goes in v2:
time: 44.2 us; the launch traced here: 44.1 us
  Pallas kernels  41.6 us (94%)
  local copies, waits for them, and re-layouts  1.88 us (4%)
  between operations  0.64 us (1%)
    pallas_call x1, Pallas kernels, on_device(): pl.pallas_call(kernel, name='section', out_shape=(jax.ShapeDtypeStruct(x....  41.6 us
    unnamed x2, local copies, waits for them, and re-layouts  1.88 us

profile of v2, /device:TPU:1, one launch (start us, length us, event | category | flops | bytes accessed | tf_op | source)
XLA Modules:
  0.0 44.1 jit_solution(1339403985206910110)
XLA Ops:
  0.6 41.6 %section.1 = (bf16[8,4096]{1,0:T(8,128)(2,1)S(1)}, bf16[924,1024]{1,0:T(8,128)(2,1)S(1)}) custom-call(bf16[8,4096]{1,0:T(8,128)(2,1)} %bitcast.23, bf16[924,128]{1,0:T(8,128)(2,1)} %bitcast.20, bf16[924,128]{1,0:T(8,128)(2,1)} %bitcast.21, bf16[924,128]{1,0:T(8,128)(2,1)} %bitcast.22, bf16[924,1024]{1,0:T(8,128)(2,1)} %bitcast.19), custom_call_target="tpu_custom_call" | custom-call | tf_op jit(solution)/shard_map/section/pallas_call | solution.py:308
  42.2 0.6 %copy.9 = bf16[1,1,8,4096]{3,2,1,0:T(8,128)(2,1)} copy(bf16[1,1,8,4096]{3,2,1,0:T(8,128)(2,1)S(1)} %bitcast.18) | data formatting | bytes 131072
  42.9 1.2 %copy.10 = bf16[1,1024,924]{1,2,0:T(8,128)(2,1)} copy(bf16[1,1024,924]{1,2,0:T(8,128)(2,1)S(1)} %bitcast.17) | data formatting | bytes 3784704

commit v3 on v2

--- a/solution.py
+++ b/solution.py
@@ -9,16 +9,21 @@
 F32 = jnp.float32
 BF16 = jnp.bfloat16
 
+RING, TREE, FLAT = (1, 1, 1, 1), (1, 1, 1, 2), (1, 2, 1, 2)
+RS_HOPS = (TREE, TREE, TREE, FLAT)
+AG_HOPS = (RING, FLAT)
+
 
 def kernel(
     x_hbm, gate_hbm, up_hbm, hid_hbm, w_hbm,
     dx_ref, dw_ref,
     gate_v, up_v, hid_v, w_v, x_v, g_all, x_all, x_mat, part, ring, fin, landed,
-    load_sem, xs, xr, ps, pr, gs, gr, ags, agr, rss, rsr, fs, fr,
+    load_sem, xs, xr, ps, pr, gs, gr, ags, agr, rss, rsr, fs, fr, turn_sem,
 ):
     p, t, y = lax.axis_index("pp"), lax.axis_index("tp"), lax.axis_index("dp")
     n_pp, n_dp = lax.axis_size("pp"), lax.axis_size("dp")
     z, xl = t // 2, lax.rem(t, 2)
+    core = lax.rem(p, 2)
     nz = 8
     hidden = gate_hbm.shape[0]
     half = g_all.shape[2]
@@ -53,14 +58,15 @@
         pltpu.make_async_copy(w_hbm, w_v, load_sem.at[3]),
         pltpu.make_async_copy(
             x_hbm.at[:, pl.ds(pl.multiple_of(y * cols, 128), cols)],
-            x_all.at[z, xl, y], load_sem.at[4]),
+            x_all.at[z, xl, 0], load_sem.at[4]),
         pltpu.make_async_copy(x_hbm, x_v, load_sem.at[5]),
     ]
     for i in (5, 0, 1, 2, 4, 3):
         loads[i].start()
 
     barrier = pltpu.get_barrier_semaphore()
-    peers = [at_y(1), at_y(2), at_y(3), at_z(1), at_z(-1), at_z(2), at_z(-2), partner]
+    peers = [at_y(1), at_y(2), at_y(3), at_z(1), at_z(-1), at_z(2), at_z(-2), partner,
+             (p + 1 - 2 * core, t, y)]
     for d in peers:
         pl.semaphore_signal(barrier, inc=1, device_id=d, device_id_type=MESH)
 
@@ -83,7 +89,7 @@
         j = ymod(y + k)
         return remote(
             x_v.at[:, pl.ds(pl.multiple_of(j * cols, 128), cols)],
-            x_all.at[z, xl, y], xs.at[k - 1], xr.at[k - 1], at_y(k))
+            x_all.at[z, xl, {1: 2, 2: 3, 3: 1}[k]], xs.at[k - 1], xr.at[k - 1], at_y(k))
 
     loads[5].wait()
     for k in (2, 1, 3):
@@ -100,63 +106,100 @@
         v = d * u * s * (1.0 + g * (1.0 - s))
         if n < half:
             v = jnp.concatenate([v, jnp.zeros((half - n, v.shape[1]), F32)], axis=0)
-        g_all[y, h] = v.astype(BF16)
+        g_all[0, h] = v.astype(BF16)
 
     def g_copy(plus, k):
-        if plus:
-            owner, h, dev = ((y, 0), (y, 1), (ymod(y - 1), 0))[k] + (at_y(1),)
-        else:
-            owner, h, dev = ((y, 1), (y, 0), (ymod(y + 1), 1))[k] + (at_y(-1),)
-        i = 0 if plus else 1
-        ref = g_all.at[owner, h]
-        return remote(ref, ref, gs.at[i, k], gr.at[i, k], dev)
-
-    for k in (0, 1):
-        go(g_copy(True, k))
-        go(g_copy(False, k))
+        i, sign = (0, 1) if plus else (1, -1)
+        near = 2 if plus else 1
+        src, dst, h = ((0, near, i), (0, near, 1 - i), (near, 3, i))[k]
+        return remote(
+            g_all.at[src, h], g_all.at[dst, h], gs.at[i, k], gr.at[i, k], at_y(sign))
+
+    def g_start():
+        for k in (0, 1):
+            g_copy(True, k).start()
+            g_copy(False, k).start()
+
+    def g_sent():
+        for k in (0, 1):
+            g_copy(True, k).wait_send()
+            g_copy(False, k).wait_send()
+
+    def g_wait(k):
+        g_copy(True, k).wait_recv()
+        g_copy(False, k).wait_recv()
+
+    def g_forward(plus):
+        g_copy(plus, 0).wait_recv()
+        go(g_copy(plus, 2))
+
+    def x_wait():
+        for k in (1, 3, 2):
+            x_copy(k).wait_recv()
+
+    @pl.when(core == 0)
+    def _():
+        g_start()
+
+    def g_pass():
+        g_sent()
+        pl.semaphore_signal(turn_sem, inc=1, device_id=(p + 1, t, y), device_id_type=MESH)
+
+    def g_turn():
+        pl.semaphore_wait(turn_sem, 1)
+        g_start()
+
+    def turn():
+        @pl.when(core == 0)
+        def _():
+            g_pass()
+
+        @pl.when(core == 1)
+        def _():
+            g_turn()
 
     def rep(ri):
         return ymod(y + (0, 1, 3, 2)[ri])
 
     def product(ri):
-        r = rep(ri)
-        g = jnp.concatenate([g_all[r, 0], g_all[r, 1]], axis=0)[:hidden]
+        g = jnp.concatenate([g_all[ri, 0], g_all[ri, 1]], axis=0)[:hidden]
         for q in range(2):
             c = pl.ds(q * hc, hc)
             acc = lax.dot_general(
                 g, w_v[:, c], (((0,), (0,)), ((), ())), preferred_element_type=F32)
             part[ri, :, :, c] = acc.astype(BF16).reshape(nz, 16, hc)
 
-    def lanes(plus):
+    def lanes(plus, m):
+        if m < 4:
+            return pl.ds(0, cols)
         return pl.ds(0, hc) if plus else pl.ds(hc, hc)
 
-    def rs_copy(plus, ri, kind):
+    def rs_copy(plus, ri, m):
         i, sign = (0, 1) if plus else (1, -1)
-        dest, hop = ((3, 1), (4, 2), (1, 1), (2, 2))[kind]
-        src = part.at[ri, zmod(z + sign * dest)]
-        dst = ring.at[i, ri, kind]
-        if kind == 1:
-            src, dst = src.at[:, lanes(plus)], dst.at[:, lanes(plus)]
-        return remote(src, dst, rss.at[i, ri, kind], rsr.at[i, ri, kind], at_z(sign * hop))
-
-    def rs_send(ri, *kinds):
-        for kind in kinds:
-            for plus in (True, False):
-                go(rs_copy(plus, ri, kind))
-
-    def rs_mid(ri):
+        c = lanes(plus, m)
+        return remote(
+            part.at[ri, zmod(z + sign * m), :, c], ring.at[i, ri, m - 1, :, c],
+            rss.at[i, ri, m - 1], rsr.at[i, ri, m - 1], at_z(sign * RS_HOPS[ri][m - 1]))
+
+    def feeds(ri, m):
+        return [n for n in range(4, m, -1) if n - RS_HOPS[ri][n - 1] == m]
+
+    def rs_send(ri, m):
         for plus in (True, False):
             i, sign = (0, 1) if plus else (1, -1)
-            for kind in (0, 1):
-                rs_copy(plus, ri, kind).wait_recv()
-            d = zmod(z + sign * 2)
-            for q in range(2):
+            came = feeds(ri, m)
+            for n in came:
+                rs_copy(plus, ri, n).wait_recv()
+            d = zmod(z + sign * m)
+            for q in range(2 if came else 0):
                 c = pl.ds(q * hc, hc)
-                v = part[ri, d, :, c].astype(F32) + ring[i, ri, 0, :, c].astype(F32)
-                if plus == (q == 0):
-                    v = v + ring[i, ri, 1, :, c].astype(F32)
-                part[ri, d, :, c] = v.astype(BF16)
-            go(rs_copy(plus, ri, 3))
+                ms = [n for n in came if n < 4 or plus == (q == 0)]
+                if ms:
+                    v = part[ri, d, :, c].astype(F32)
+                    for n in ms:
+                        v = v + ring[i, ri, n - 1, :, c].astype(F32)
+                    part[ri, d, :, c] = v.astype(BF16)
+            go(rs_copy(plus, ri, m))
 
     def fin_copy(ri, xq):
         return remote(
@@ -165,10 +208,10 @@
 
     def rs_end(ri):
         v = part[ri, z].astype(F32)
-        for kind in (2, 3):
+        for m in feeds(ri, 0):
             for plus in (True, False):
-                rs_copy(plus, ri, kind).wait_recv()
-                v = v + ring[0 if plus else 1, ri, kind].astype(F32)
+                rs_copy(plus, ri, m).wait_recv()
+                v = v + ring[0 if plus else 1, ri, m - 1].astype(F32)
         v = v.reshape(2, 8, cols).astype(BF16)
         for xq in range(2):
             fin[ri, xq] = v[xq]
@@ -178,75 +221,89 @@
             for xq in range(2):
                 fin_copy(ri, xq).start()
 
+    def pair_send(k):
+        go(pair_copy(k))
+
     def pair_copy(k):
         ref = x_all.at[zmod(z + k), xl]
         return remote(ref, ref, ps.at[k % nz], pr.at[k % nz], partner)
 
-    def ag_copy(plus, kind):
-        i, sign = (0, 1) if plus else (1, -1)
-        origin, hop = ((0, 1), (0, 2), (-2, 1), (-2, 2))[kind]
-        ref = x_all.at[zmod(z + sign * origin), xl]
-        if kind == 3:
-            ref = ref.at[pl.ds(0, 2)] if plus else ref.at[pl.ds(2, 2)]
-        return remote(ref, ref, ags.at[i, kind], agr.at[i, kind], at_z(sign * hop))
-
-    def ag_send(*kinds):
-        for kind in kinds:
-            for plus in (True, False):
-                go(ag_copy(plus, kind))
-
-    def ag_wait(kind):
+    def ag_copies(g, k):
+        out = []
         for plus in (True, False):
-            ag_copy(plus, kind).wait_recv()
-
+            i, sign = (0, 1) if plus else (1, -1)
+            lo, n = ((0, 1), (1, 3))[g]
+            if k == 4:
+                lo, n = (((0, 1), (1, 1)) if plus else ((0, 0), (2, 2)))[g]
+            if n == 0:
+                continue
+            hop = AG_HOPS[g][k - 1]
+            ref = x_all.at[zmod(z - sign * (k - hop)), xl, pl.ds(lo, n)]
+            out.append(remote(
+                ref, ref, ags.at[g, i, k - 1], agr.at[g, i, k - 1], at_z(sign * hop)))
+        return out
+
+    def ag_send(g, k):
+        for c in ag_copies(g, k):
+            go(c)
+
+    def ag_wait(g, k):
+        for c in ag_copies(g, k):
+            c.wait_recv()
+
+    loads[4].wait()
     loads[3].wait()
     product(0)
-    rs_send(0, 1, 0)
-
-    loads[4].wait()
-    for k in (1, 3, 2):
-        x_copy(k).wait_recv()
-    ag_send(1, 0)
-    go(pair_copy(0))
+    rs_send(0, 3)
+    rs_send(0, 4)
+    ag_send(0, 1)
+    x_wait()
+    ag_send(1, 2)
+    ag_wait(0, 1)
+    ag_send(0, 2)
+    turn()
+    pair_send(0)
+    ag_send(1, 1)
+    g_forward(False)
+    g_forward(True)
     rs_send(0, 2)
-
-    rs_mid(0)
-    g_copy(True, 0).wait_recv()
-    go(g_copy(True, 2))
-    g_copy(False, 0).wait_recv()
-    go(g_copy(False, 2))
-
-    ag_wait(1)
-    ag_send(3, 2)
-    go(pair_copy(2))
-    go(pair_copy(-2))
-
-    g_copy(True, 1).wait_recv()
-    g_copy(False, 1).wait_recv()
+    g_wait(1)
     product(1)
-    rs_send(1, 1, 0)
+    rs_send(1, 4)
     product(2)
-    rs_send(2, 1, 0)
-    ag_wait(0)
-    go(pair_copy(1))
-    go(pair_copy(-1))
+    rs_send(2, 3)
+    rs_send(1, 3)
+    rs_send(2, 4)
+    ag_wait(0, 2)
+    ag_wait(1, 2)
+    pair_send(2)
+    pair_send(-2)
+    ag_send(1, 3)
+    ag_send(0, 3)
+    ag_send(1, 4)
+    g_wait(2)
+    product(3)
+    rs_send(3, 4)
+    ag_wait(1, 1)
+    pair_send(1)
+    pair_send(-1)
+    rs_send(1, 2)
+    rs_send(3, 3)
+    rs_send(2, 2)
+    rs_send(3, 1)
+    ag_wait(0, 3)
+    ag_wait(1, 3)
+    pair_send(3)
+    pair_send(-3)
+    ag_send(0, 4)
+    rs_send(0, 1)
+    rs_send(1, 1)
+    rs_send(3, 2)
+    rs_send(2, 1)
+    ag_wait(0, 4)
+    ag_wait(1, 4)
+    pair_send(4)
     rs_end(0)
-
-    g_copy(True, 2).wait_recv()
-    g_copy(False, 2).wait_recv()
-    product(3)
-    rs_send(3, 1, 0)
-    rs_send(1, 2)
-    rs_send(2, 2)
-    rs_send(3, 2)
-    rs_mid(1)
-    rs_mid(2)
-    ag_wait(2)
-    go(pair_copy(3))
-    go(pair_copy(-3))
-    ag_wait(3)
-    go(pair_copy(4))
-    rs_mid(3)
     rs_end(1)
     rs_end(2)
     rs_end(3)
@@ -288,6 +345,11 @@
 
     for c in sends:
         c.wait_send()
+
+    @pl.when(core == 1)
+    def _():
+        g_sent()
+
 
     @pl.when(p > 0)
     def _():
@@ -327,9 +389,9 @@
             vm((4, 2, 8, cols), BF16),
             dma((6,)), dma((3,)), dma((3,)), dma((8,)), dma((8,)),
             dma((2, 3)), dma((2, 3)),
-            dma((2, 4)), dma((2, 4)),
+            dma((2, 2, 4)), dma((2, 2, 4)),
             dma((2, 4, 4)), dma((2, 4, 4)),
-            dma((4, 2)), dma((4, 2)),
+            dma((4, 2)), dma((4, 2)), pltpu.SemaphoreType.REGULAR,
         ],
         compiler_params=pltpu.CompilerParams(
             collective_id=0, has_side_effects=True, vmem_limit_bytes=40 << 20),

time: 44.2 us -> 40.3 us (0.912)
  Pallas kernels: 41.6 us -> 37.7 us
    pallas_call x1, Pallas kernels: 41.6 us -> 37.7 us  [on_device(): pl.pallas_call(kernel, name='section', out_shape=(jax.ShapeDtypeStruct(x....]
where the time goes in v3:
time: 40.3 us; the launch traced here: 40.2 us
  Pallas kernels  37.7 us (94%)
  local copies, waits for them, and re-layouts  1.88 us (5%)
  between operations  0.64 us (2%)
    pallas_call x1, Pallas kernels, on_device(): pl.pallas_call(kernel, name='section', out_shape=(jax.ShapeDtypeStruct(x....  37.7 us
    unnamed x2, local copies, waits for them, and re-layouts  1.88 us

profile of v3, /device:TPU:1, one launch (start us, length us, event | category | flops | bytes accessed | tf_op | source)
XLA Modules:
  0.0 40.2 jit_solution(8101418803312883577)
XLA Ops:
  0.6 37.7 %section.1 = (bf16[8,4096]{1,0:T(8,128)(2,1)S(1)}, bf16[924,1024]{1,0:T(8,128)(2,1)S(1)}) custom-call(bf16[8,4096]{1,0:T(8,128)(2,1)} %bitcast.23, bf16[924,128]{1,0:T(8,128)(2,1)} %bitcast.20, bf16[924,128]{1,0:T(8,128)(2,1)} %bitcast.21, bf16[924,128]{1,0:T(8,128)(2,1)} %bitcast.22, bf16[924,1024]{1,0:T(8,128)(2,1)} %bitcast.19), custom_call_target="tpu_custom_call" | custom-call | tf_op jit(solution)/shard_map/section/pallas_call | solution.py:370
  38.3 0.6 %copy.9 = bf16[1,1,8,4096]{3,2,1,0:T(8,128)(2,1)} copy(bf16[1,1,8,4096]{3,2,1,0:T(8,128)(2,1)S(1)} %bitcast.18) | data formatting | bytes 131072
  38.9 1.2 %copy.10 = bf16[1,1024,924]{1,2,0:T(8,128)(2,1)} copy(bf16[1,1024,924]{1,2,0:T(8,128)(2,1)S(1)} %bitcast.17) | data formatting | bytes 3784704

commit v4 on v3

--- a/solution.py
+++ b/solution.py
@@ -10,8 +10,11 @@
 BF16 = jnp.bfloat16
 
 RING, TREE, FLAT = (1, 1, 1, 1), (1, 1, 1, 2), (1, 2, 1, 2)
-RS_HOPS = (TREE, TREE, TREE, FLAT)
-AG_HOPS = (RING, FLAT)
+RS_HOPS = (
+    (FLAT, FLAT, TREE, FLAT),
+    (FLAT, TREE, RING, FLAT),
+)
+AG_HOPS = ((FLAT, FLAT), (TREE, TREE))
 
 
 def kernel(
@@ -79,11 +82,10 @@
 
     pl.semaphore_wait(barrier, jnp.where(p > 0, len(peers) + 8, len(peers)))
 
-    sends = []
+    side = [0]
 
     def go(c):
         c.start()
-        sends.append(c)
 
     def x_copy(k):
         j = ymod(y + k)
@@ -120,17 +122,15 @@
             g_copy(True, k).start()
             g_copy(False, k).start()
 
-    def g_sent():
-        for k in (0, 1):
+    def g_sent(*ks):
+        for k in ks:
             g_copy(True, k).wait_send()
             g_copy(False, k).wait_send()
 
-    def g_wait(k):
-        g_copy(True, k).wait_recv()
-        g_copy(False, k).wait_recv()
+    def g_recv(plus, k):
+        g_copy(plus, k).wait_recv()
 
     def g_forward(plus):
-        g_copy(plus, 0).wait_recv()
         go(g_copy(plus, 2))
 
     def x_wait():
@@ -142,21 +142,12 @@
         g_start()
 
     def g_pass():
-        g_sent()
+        g_sent(0)
         pl.semaphore_signal(turn_sem, inc=1, device_id=(p + 1, t, y), device_id_type=MESH)
 
     def g_turn():
         pl.semaphore_wait(turn_sem, 1)
         g_start()
-
-    def turn():
-        @pl.when(core == 0)
-        def _():
-            g_pass()
-
-        @pl.when(core == 1)
-        def _():
-            g_turn()
 
     def rep(ri):
         return ymod(y + (0, 1, 3, 2)[ri])
@@ -179,10 +170,10 @@
         c = lanes(plus, m)
         return remote(
             part.at[ri, zmod(z + sign * m), :, c], ring.at[i, ri, m - 1, :, c],
-            rss.at[i, ri, m - 1], rsr.at[i, ri, m - 1], at_z(sign * RS_HOPS[ri][m - 1]))
+            rss.at[i, ri, m - 1], rsr.at[i, ri, m - 1], at_z(sign * RS_HOPS[side[0]][ri][m - 1]))
 
     def feeds(ri, m):
-        return [n for n in range(4, m, -1) if n - RS_HOPS[ri][n - 1] == m]
+        return [n for n in range(4, m, -1) if n - RS_HOPS[side[0]][ri][n - 1] == m]
 
     def rs_send(ri, m):
         for plus in (True, False):
@@ -237,7 +228,7 @@
                 lo, n = (((0, 1), (1, 1)) if plus else ((0, 0), (2, 2)))[g]
             if n == 0:
                 continue
-            hop = AG_HOPS[g][k - 1]
+            hop = AG_HOPS[side[0]][g][k - 1]
             ref = x_all.at[zmod(z - sign * (k - hop)), xl, pl.ds(lo, n)]
             out.append(remote(
                 ref, ref, ags.at[g, i, k - 1], agr.at[g, i, k - 1], at_z(sign * hop)))
@@ -252,61 +243,134 @@
             c.wait_recv()
 
     loads[4].wait()
-    loads[3].wait()
-    product(0)
-    rs_send(0, 3)
-    rs_send(0, 4)
-    ag_send(0, 1)
-    x_wait()
-    ag_send(1, 2)
-    ag_wait(0, 1)
-    ag_send(0, 2)
-    turn()
-    pair_send(0)
-    ag_send(1, 1)
-    g_forward(False)
-    g_forward(True)
-    rs_send(0, 2)
-    g_wait(1)
-    product(1)
-    rs_send(1, 4)
-    product(2)
-    rs_send(2, 3)
-    rs_send(1, 3)
-    rs_send(2, 4)
-    ag_wait(0, 2)
-    ag_wait(1, 2)
-    pair_send(2)
-    pair_send(-2)
-    ag_send(1, 3)
-    ag_send(0, 3)
-    ag_send(1, 4)
-    g_wait(2)
-    product(3)
-    rs_send(3, 4)
-    ag_wait(1, 1)
-    pair_send(1)
-    pair_send(-1)
-    rs_send(1, 2)
-    rs_send(3, 3)
-    rs_send(2, 2)
-    rs_send(3, 1)
-    ag_wait(0, 3)
-    ag_wait(1, 3)
-    pair_send(3)
-    pair_send(-3)
-    ag_send(0, 4)
-    rs_send(0, 1)
-    rs_send(1, 1)
-    rs_send(3, 2)
-    rs_send(2, 1)
-    ag_wait(0, 4)
-    ag_wait(1, 4)
-    pair_send(4)
-    rs_end(0)
-    rs_end(1)
-    rs_end(2)
-    rs_end(3)
+
+    @pl.when(core == 0)
+    def _():
+        side[0] = 0
+        loads[3].wait()
+        product(0)
+        rs_send(0, 3)
+        rs_send(0, 4)
+        rs_send(0, 1)
+        ag_send(0, 2)
+        g_pass()
+        ag_send(0, 1)
+        x_wait()
+        ag_send(1, 2)
+        rs_send(0, 2)
+        ag_wait(0, 2)
+        ag_send(0, 4)
+        g_recv(True, 0)
+        g_forward(True)
+        g_recv(False, 0)
+        g_forward(False)
+        ag_send(1, 1)
+        g_recv(False, 1)
+        product(1)
+        g_recv(True, 1)
+        product(2)
+        rs_send(1, 4)
+        rs_send(2, 4)
+        rs_send(2, 3)
+        rs_send(1, 3)
+        ag_wait(1, 2)
+        ag_send(1, 4)
+        pair_send(2)
+        pair_send(-2)
+        ag_send(1, 3)
+        pair_send(0)
+        g_recv(True, 2)
+        g_recv(False, 2)
+        product(3)
+        rs_send(3, 4)
+        ag_send(0, 3)
+        rs_send(3, 3)
+        rs_end(0)
+        rs_send(2, 2)
+        rs_send(1, 2)
+        ag_wait(0, 4)
+        ag_wait(1, 4)
+        pair_send(4)
+        ag_wait(0, 1)
+        ag_wait(1, 1)
+        pair_send(1)
+        pair_send(-1)
+        rs_send(1, 1)
+        rs_send(3, 2)
+        rs_send(3, 1)
+        ag_wait(0, 3)
+        ag_wait(1, 3)
+        pair_send(3)
+        pair_send(-3)
+        rs_send(2, 1)
+        rs_end(3)
+        rs_end(1)
+        rs_end(2)
+
+    @pl.when(core == 1)
+    def _():
+        side[0] = 1
+        ag_send(0, 1)
+        loads[3].wait()
+        product(0)
+        rs_send(0, 1)
+        rs_send(0, 4)
+        ag_wait(0, 1)
+        ag_send(0, 2)
+        rs_send(0, 3)
+        x_wait()
+        ag_send(1, 1)
+        g_turn()
+        rs_send(0, 2)
+        g_recv(False, 0)
+        g_recv(False, 1)
+        product(1)
+        g_recv(True, 0)
+        g_recv(True, 1)
+        product(2)
+        ag_wait(1, 1)
+        ag_send(1, 2)
+        rs_send(2, 4)
+        pair_send(1)
+        pair_send(-1)
+        g_forward(False)
+        rs_send(1, 3)
+        g_forward(True)
+        g_recv(True, 2)
+        g_recv(False, 2)
+        product(3)
+        rs_send(1, 4)
+        rs_send(2, 3)
+        rs_send(3, 3)
+        rs_send(3, 4)
+        rs_send(1, 2)
+        ag_wait(0, 2)
+        ag_send(0, 3)
+        ag_wait(1, 2)
+        pair_send(2)
+        pair_send(-2)
+        pair_send(0)
+        ag_send(1, 3)
+        rs_send(2, 2)
+        ag_send(1, 4)
+        ag_send(0, 4)
+        rs_send(3, 2)
+        rs_send(3, 1)
+        rs_end(0)
+        rs_send(1, 1)
+        ag_wait(0, 3)
+        ag_wait(1, 3)
+        pair_send(3)
+        pair_send(-3)
+        rs_send(2, 1)
+        ag_wait(0, 4)
+        ag_wait(1, 4)
+        pair_send(4)
+        rs_end(3)
+        rs_end(1)
+        rs_end(2)
+
+    side[0] = 0
 
     for k in range(nz):
         pair_copy(k).wait_recv()
@@ -343,12 +407,25 @@
     def _():
         dx_ref[...] = jnp.zeros_like(dx_ref)
 
-    for c in sends:
-        c.wait_send()
+    for k in (1, 2, 3):
+        x_copy(k).wait_send()
+    for k in range(nz):
+        pair_copy(k).wait_send()
+    for k in range(1, 5):
+        for g in range(2):
+            for c in ag_copies(g, k):
+                c.wait_send()
+        for plus in (True, False):
+            for ri in range(4):
+                rs_copy(plus, ri, k).wait_send()
+    for plus in (True, False):
+        g_copy(plus, 2).wait_send()
+
+    g_sent(1)
 
     @pl.when(core == 1)
     def _():
-        g_sent()
+        g_sent(0)
 
 
     @pl.when(p > 0)
@@ -356,6 +433,17 @@
         for ri in range(4):
             for xq in range(2):
                 fin_copy(ri, xq).wait_send()
+
+
+def write_out(dx_v, dw_v, dx_hbm, dw_hbm, sem):
+    copies = [
+        pltpu.make_async_copy(dw_v, dw_hbm, sem.at[0]),
+        pltpu.make_async_copy(dx_v, dx_hbm, sem.at[1]),
+    ]
+    for c in copies:
+        c.start()
+    for c in copies:
+        c.wait()
 
 
 def on_device(layer_input, gate_pre, up_pre, hidden_grad, gate_weight):
@@ -396,6 +484,18 @@
         compiler_params=pltpu.CompilerParams(
             collective_id=0, has_side_effects=True, vmem_limit_bytes=40 << 20),
     )(*(pltpu.with_memory_space_constraint(v, pltpu.HBM) for v in (x, gate, up, hid, w)))
+    dx, dw = pl.pallas_call(
+        write_out,
+        name="write_out",
+        out_shape=(
+            jax.ShapeDtypeStruct(x.shape, BF16),
+            jax.ShapeDtypeStruct((hidden, cols), BF16),
+        ),
+        in_specs=[pl.BlockSpec(memory_space=pltpu.VMEM)] * 2,
+        out_specs=[pl.BlockSpec(memory_space=pltpu.HBM)] * 2,
+        scratch_shapes=[dma((2,))],
+        compiler_params=pltpu.CompilerParams(vmem_limit_bytes=8 << 20),
+    )(dx, dw)
     return dx[None, None], jnp.swapaxes(dw, 0, 1)[None]
 
 

time: 40.3 us -> 38.3 us (0.950)
  local copies, waits for them, and re-layouts: 1.88 us -> 0 us
    unnamed x2 -> x0, local copies, waits for them, and re-layouts: 1.88 us -> none
    pallas_call x1, Pallas kernels: 37.7 us -> 36.3 us  [on_device(): pl.pallas_call(kernel, name='section', out_shape=(jax.ShapeDtypeStruct(x....]
    pallas_call x0 -> x1, Pallas kernels: none -> 1.27 us  [on_device(): pl.pallas_call(write_out, name='write_out', out_shape=(jax.ShapeDtypeStru...]
where the time goes in v4:
time: 38.3 us; the launch traced here: 38.2 us
  Pallas kernels  37.6 us (98%)
  between operations  0.64 us (2%)
    pallas_call x1, Pallas kernels, on_device(): pl.pallas_call(kernel, name='section', out_shape=(jax.ShapeDtypeStruct(x....  36.3 us
    pallas_call x1, Pallas kernels, on_device(): pl.pallas_call(write_out, name='write_out', out_shape=(jax.ShapeDtypeStru...  1.27 us

profile of v4, /device:TPU:1, one launch (start us, length us, event | category | flops | bytes accessed | tf_op | source)
XLA Modules:
  0.0 38.2 jit_solution(12731928710464374097)
XLA Ops:
  0.6 36.3 %section.1 = (bf16[8,4096]{1,0:T(8,128)(2,1)S(1)}, bf16[924,1024]{1,0:T(8,128)(2,1)S(1)}) custom-call(bf16[8,4096]{1,0:T(8,128)(2,1)} %bitcast.21, bf16[924,128]{1,0:T(8,128)(2,1)} %bitcast.18, bf16[924,128]{1,0:T(8,128)(2,1)} %bitcast.19, bf16[924,128]{1,0:T(8,128)(2,1)} %bitcast.20, bf16[924,1024]{1,0:T(8,128)(2,1)} %bitcast.17), custom_call_target="tpu_custom_call" | custom-call | tf_op jit(solution)/shard_map/section/pallas_call | solution.py:458
  36.9 1.3 %write_out.1 = (bf16[8,4096]{1,0:T(8,128)(2,1)}, bf16[924,1024]{1,0:T(8,128)(2,1)}) custom-call(bf16[8,4096]{1,0:T(8,128)(2,1)S(1)} %get-tuple-element.6.dx_v, bf16[924,1024]{1,0:T(8,128)(2,1)S(1)} %get-tuple-element.7.dw_v), custom_call_target="tpu_custom_call" | custom-call | tf_op jit(solution)/shard_map/write_out/pallas_call | solution.py:487

commit v5 on v4

--- a/solution.py
+++ b/solution.py
@@ -257,13 +257,13 @@
         ag_send(0, 1)
         x_wait()
         ag_send(1, 2)
-        rs_send(0, 2)
-        ag_wait(0, 2)
-        ag_send(0, 4)
         g_recv(True, 0)
         g_forward(True)
         g_recv(False, 0)
         g_forward(False)
+        rs_send(0, 2)
+        ag_wait(0, 2)
+        ag_send(0, 4)
         ag_send(1, 1)
         g_recv(False, 1)
         product(1)
@@ -320,12 +320,15 @@
         rs_send(0, 3)
         x_wait()
         ag_send(1, 1)
+        pair_send(0)
         g_turn()
         rs_send(0, 2)
+        g_recv(True, 0)
+        g_forward(True)
         g_recv(False, 0)
+        g_forward(False)
         g_recv(False, 1)
         product(1)
-        g_recv(True, 0)
         g_recv(True, 1)
         product(2)
         ag_wait(1, 1)
@@ -333,9 +336,7 @@
         rs_send(2, 4)
         pair_send(1)
         pair_send(-1)
-        g_forward(False)
         rs_send(1, 3)
-        g_forward(True)
         g_recv(True, 2)
         g_recv(False, 2)
         product(3)
@@ -343,14 +344,13 @@
         rs_send(2, 3)
         rs_send(3, 3)
         rs_send(3, 4)
-        rs_send(1, 2)
         ag_wait(0, 2)
         ag_send(0, 3)
         ag_wait(1, 2)
+        ag_send(1, 3)
         pair_send(2)
         pair_send(-2)
-        pair_send(0)
-        ag_send(1, 3)
+        rs_send(1, 2)
         rs_send(2, 2)
         ag_send(1, 4)
         ag_send(0, 4)

time: 38.3 us -> 38.1 us (level)
  no operation moved by 1% of the time
where the time goes in v5:
time: 38.1 us; the launch traced here: 38 us
  Pallas kernels  37.4 us (98%)
  between operations  0.64 us (2%)
    pallas_call x1, Pallas kernels, on_device(): pl.pallas_call(kernel, name='section', out_shape=(jax.ShapeDtypeStruct(x....  36.1 us
    pallas_call x1, Pallas kernels, on_device(): pl.pallas_call(write_out, name='write_out', out_shape=(jax.ShapeDtypeStru...  1.27 us

profile of v5, /device:TPU:1, one launch (start us, length us, event | category | flops | bytes accessed | tf_op | source)
XLA Modules:
  0.0 38.0 jit_solution(10847292013811986068)
XLA Ops:
  0.6 36.1 %section.1 = (bf16[8,4096]{1,0:T(8,128)(2,1)S(1)}, bf16[924,1024]{1,0:T(8,128)(2,1)S(1)}) custom-call(bf16[8,4096]{1,0:T(8,128)(2,1)} %bitcast.21, bf16[924,128]{1,0:T(8,128)(2,1)} %bitcast.18, bf16[924,128]{1,0:T(8,128)(2,1)} %bitcast.19, bf16[924,128]{1,0:T(8,128)(2,1)} %bitcast.20, bf16[924,1024]{1,0:T(8,128)(2,1)} %bitcast.17), custom_call_target="tpu_custom_call" | custom-call | tf_op jit(solution)/shard_map/section/pallas_call | solution.py:458
  36.8 1.3 %write_out.1 = (bf16[8,4096]{1,0:T(8,128)(2,1)}, bf16[924,1024]{1,0:T(8,128)(2,1)}) custom-call(bf16[8,4096]{1,0:T(8,128)(2,1)S(1)} %get-tuple-element.6.dx_v, bf16[924,1024]{1,0:T(8,128)(2,1)S(1)} %get-tuple-element.7.dw_v), custom_call_target="tpu_custom_call" | custom-call | tf_op jit(solution)/shard_map/write_out/pallas_call | solution.py:487
